TPU v7x, 32 devices: a whole 2x2x4 slice. The times are simulated.
32 devices in a mesh: dp: 8 (over y, x, core), tensor: 4 (over z).
Axes of the slice: x: 2, y: 2, z: 4, core: 2. Of those that a mesh axis runs over, the one named last changes fastest.
Arguments:
- tokens_in: bfloat16 [8192, 1536], P('dp'), may hold values from -6 to 6
- doc_ids: int32 [8192], replicated, may hold values from 0 to 3, never falling along the last dimension, each value on 1 to 4096 neighbouring positions
- out_grad: bfloat16 [8192, 1536], P('dp'), may hold values from -6 to 6
- norm_gains: bfloat16 [2, 1536], replicated, may hold values from 0.5 to 1.5
- conv_taps: bfloat16 [3, 1536], P(None, 'tensor'), may hold values from -3.5 to 3.5
- stream_weight: bfloat16 [3, 1536, 1536], P(None, None, 'tensor'), may hold values from -0.15625 to 0.15625
- mixer_weight: bfloat16 [1536, 1536], P('tensor'), may hold values from -0.15625 to 0.15625
- hidden_weight: bfloat16 [2, 1536, 6912], P(None, None, 'tensor'), may hold values from -0.15625 to 0.15625
- down_weight: bfloat16 [6912, 1536], P('tensor'), may hold values from -0.078125 to 0.078125
- gains_first: float32 [2, 1536], replicated, may hold values from -0.0009336855 to 0.0009336855
- gains_second: float32 [2, 1536], replicated, may hold values from 7.2647386e-09 to 7.264739e-08
- taps_first: float32 [3, 1536], P(None, 'tensor'), may hold values from -0.0009336855 to 0.0009336855
- taps_second: float32 [3, 1536], P(None, 'tensor'), may hold values from 7.2647386e-09 to 7.264739e-08
- stream_first: float32 [3, 1536, 1536], P(None, 'dp', 'tensor'), may hold values from -0.0009336855 to 0.0009336855
- stream_second: float32 [3, 1536, 1536], P(None, 'dp', 'tensor'), may hold values from 7.2647386e-09 to 7.264739e-08
- mixer_first: float32 [1536, 1536], P('tensor', 'dp'), may hold values from -0.0009336855 to 0.0009336855
- mixer_second: float32 [1536, 1536], P('tensor', 'dp'), may hold values from 7.2647386e-09 to 7.264739e-08
- hidden_first: float32 [2, 1536, 6912], P(None, 'dp', 'tensor'), may hold values from -0.0009336855 to 0.0009336855
- hidden_second: float32 [2, 1536, 6912], P(None, 'dp', 'tensor'), may hold values from 7.2647386e-09 to 7.264739e-08
- down_first: float32 [6912, 1536], P('tensor', 'dp'), may hold values from -0.0009336855 to 0.0009336855
- down_second: float32 [6912, 1536], P('tensor', 'dp'), may hold values from 7.2647386e-09 to 7.264739e-08
Outputs:
- block_out: bfloat16 [8192, 1536], P('dp')
- input_grad: float32 [8192, 1536], P('dp')
- grad_norm: float32 [], replicated
- gains_grad: float32 [2, 1536], replicated
- gains_first_next: float32 [2, 1536], replicated
- gains_second_next: float32 [2, 1536], replicated
- gains_step: float32 [2, 1536], replicated
- taps_grad: float32 [3, 1536], P(None, 'tensor')
- taps_first_next: float32 [3, 1536], P(None, 'tensor')
- taps_second_next: float32 [3, 1536], P(None, 'tensor')
- taps_step: float32 [3, 1536], P(None, 'tensor')
- stream_grad: float32 [3, 1536, 1536], P(None, 'dp', 'tensor')
- stream_first_next: float32 [3, 1536, 1536], P(None, 'dp', 'tensor')
- stream_second_next: float32 [3, 1536, 1536], P(None, 'dp', 'tensor')
- stream_step: float32 [3, 1536, 1536], P(None, 'dp', 'tensor')
- mixer_grad: float32 [1536, 1536], P('tensor', 'dp')
- mixer_first_next: float32 [1536, 1536], P('tensor', 'dp')
- mixer_second_next: float32 [1536, 1536], P('tensor', 'dp')
- mixer_step: float32 [1536, 1536], P('tensor', 'dp')
- hidden_grad: float32 [2, 1536, 6912], P(None, 'dp', 'tensor')
- hidden_first_next: float32 [2, 1536, 6912], P(None, 'dp', 'tensor')
- hidden_second_next: float32 [2, 1536, 6912], P(None, 'dp', 'tensor')
- hidden_step: float32 [2, 1536, 6912], P(None, 'dp', 'tensor')
- down_grad: float32 [6912, 1536], P('tensor', 'dp')
- down_first_next: float32 [6912, 1536], P('tensor', 'dp')
- down_second_next: float32 [6912, 1536], P('tensor', 'dp')
- down_step: float32 [6912, 1536], P('tensor', 'dp')
Inputs may be any that keep to these rules, and one draw needn't show every extreme that they name: `doc_ids`: document ids never fall along the tokens; each document has 1 to 4096 tokens, and one has exactly 4096.
All inputs are finite; a program needn't handle non-finite values.
Results may differ from a plain program's by a relative error of at most 0.01.
The roundings to bfloat16 on the way count: a program that leaves them out, or rounds other values in their place, can miss the bound.
Values may be sent and summed in bfloat16 or wider, within the bound.
A program may use at most 256 MiB of HBM per device.

v0:
```python
import jax
import jax.numpy as jnp
from jax import lax
from jax.sharding import PartitionSpec as P

EPS_NORM = 1e-05
LEARN_RATE = 0.02
BETA_FIRST = 0.5
BETA_SECOND = 0.5
CORRECTION = 1.0 - 0.5**3
ADAM_EPS = 1e-08
DECAY_RATE = 0.1
CLIP_NORM = 1.0


def shifted(value, axis, steps):
    count = lax.axis_size(axis)
    leading, last = (max(0, -steps), min(count, count - steps))
    return lax.ppermute(value, axis, [(source, source + steps) for source in range(leading, last)])


def rms_scale(values):
    return lax.rsqrt(jnp.mean(values * values, axis=-1, keepdims=True) + EPS_NORM)


def norm_back(grad_normed, normal, inverse, gain_row):
    scaled = grad_normed * gain_row
    return inverse * (scaled - normal * jnp.mean(scaled * normal, axis=-1, keepdims=True))


def adam_step(master, gradient, first_moment, second_moment, factor, decay):
    clipped = gradient * factor
    first_next = BETA_FIRST * first_moment + (1.0 - BETA_FIRST) * clipped
    second_next = BETA_SECOND * second_moment + (1.0 - BETA_SECOND) * clipped * clipped
    change = -LEARN_RATE * (
        first_next / CORRECTION / (jnp.sqrt(second_next / CORRECTION) + ADAM_EPS) + decay * master
    )
    return (first_next, second_next, change)


def own_share(weight, share):
    offset_row = lax.axis_index("dp") * share
    return lax.dynamic_slice_in_dim(weight, offset_row, share, 1).astype(jnp.float32)


def contract_rows(left, right):
    return lax.dot_general(
        left, right, (((0,), (0,)), ((), ())), preferred_element_type=jnp.float32
    )


def contract_cols(left, right):
    return lax.dot_general(
        left, right, (((1,), (1,)), ((), ())), preferred_element_type=jnp.float32
    )


def squares(values):
    return jnp.sum(values * values)


def body(
    tokens_in,
    doc_ids,
    out_grad,
    norm_gains,
    conv_taps,
    stream_weight,
    mixer_weight,
    hidden_weight,
    down_weight,
    gains_first,
    gains_second,
    taps_first,
    taps_second,
    stream_first,
    stream_second,
    mixer_first,
    mixer_second,
    hidden_first,
    hidden_second,
    down_first,
    down_second,
):
    tok_rows = tokens_in.shape[0]
    kernel = conv_taps.shape[0]
    reach = kernel - 1
    first_row = lax.axis_index("dp") * tok_rows
    filler = jnp.full((reach,), -1, jnp.int32)
    padded_ids = jnp.concatenate([filler, doc_ids, filler])
    window = lax.dynamic_slice_in_dim(padded_ids, first_row, tok_rows + 2 * reach)
    current = window[reach : reach + tok_rows]
    back_valid = [
        (window[reach - offset : reach - offset + tok_rows] == current).astype(jnp.float32)[:, None]
        for offset in range(kernel)
    ]
    ahead_valid = [
        (window[reach + offset : reach + offset + tok_rows] == current).astype(jnp.float32)[:, None]
        for offset in range(kernel)
    ]
    tokens = tokens_in.astype(jnp.float32)
    gain_pair = norm_gains.astype(jnp.float32)
    tap_values = conv_taps.astype(jnp.float32)
    scale_one = rms_scale(tokens)
    normal_one = tokens * scale_one
    normed_one = (normal_one * gain_pair[0]).astype(jnp.bfloat16)
    streams = jnp.einsum(
        "td,sdc->stc", normed_one, stream_weight, preferred_element_type=jnp.float32
    )
    product = (streams[0] * streams[2]).astype(jnp.bfloat16)
    edge_rows = shifted(product[tok_rows - reach :], "dp", 1)
    extended = jnp.concatenate([edge_rows, product], 0).astype(jnp.float32)
    conv_out = tap_values[0] * extended[reach : reach + tok_rows] * back_valid[0]
    for offset in range(1, kernel):
        conv_out = (
            conv_out
            + tap_values[offset]
            * extended[reach - offset : reach - offset + tok_rows]
            * back_valid[offset]
        )
    gated_rows = (streams[1] * conv_out).astype(jnp.bfloat16)
    branch_part = jnp.dot(gated_rows, mixer_weight, preferred_element_type=jnp.float32)
    branch = lax.psum(branch_part, "tensor")
    middle = tokens + branch
    scale_two = rms_scale(middle)
    normal_two = middle * scale_two
    normed_two = (normal_two * gain_pair[1]).astype(jnp.bfloat16)
    hidden = jnp.einsum(
        "td,sdf->stf", normed_two, hidden_weight, preferred_element_type=jnp.float32
    )
    sigmoid_gate = jax.nn.sigmoid(hidden[0])
    silu_gate = hidden[0] * sigmoid_gate
    active = (silu_gate * hidden[1]).astype(jnp.bfloat16)
    feed_part = jnp.dot(active, down_weight, preferred_element_type=jnp.float32)
    feed_out = lax.psum(feed_part.astype(jnp.bfloat16), "tensor").astype(jnp.float32)
    block_out = (middle + feed_out).astype(jnp.bfloat16)
    upstream = out_grad.astype(jnp.float32)
    down_part = contract_rows(active, out_grad)
    grad_active = contract_cols(out_grad, down_weight)
    grad_gate = grad_active * hidden[1] * sigmoid_gate * (1.0 + hidden[0] * (1.0 - sigmoid_gate))
    grad_up = grad_active * silu_gate
    grad_hidden = jnp.stack([grad_gate, grad_up]).astype(jnp.bfloat16)
    hidden_part = jnp.einsum(
        "td,stf->sdf", normed_two, grad_hidden, preferred_element_type=jnp.float32
    )
    normed_two_part = jnp.einsum(
        "stf,sdf->td", grad_hidden, hidden_weight, preferred_element_type=jnp.float32
    )
    grad_normed_two = lax.psum(normed_two_part, "tensor")
    gain_two_part = jnp.sum(grad_normed_two * normal_two, axis=0)
    grad_middle = upstream + norm_back(grad_normed_two, normal_two, scale_two, gain_pair[1])
    grad_branch = grad_middle.astype(jnp.bfloat16)
    mixer_part = contract_rows(gated_rows, grad_branch)
    grad_gated = contract_cols(grad_branch, mixer_weight)
    grad_c = grad_gated * conv_out
    grad_conv = (grad_gated * streams[1]).astype(jnp.bfloat16)
    ahead_rows = shifted(grad_conv[:reach], "dp", -1)
    trailing = jnp.concatenate([grad_conv, ahead_rows], 0).astype(jnp.float32)
    grad_conv_wide = trailing[:tok_rows]
    taps_part = jnp.stack(
        [
            jnp.sum(
                grad_conv_wide
                * extended[reach - offset : reach - offset + tok_rows]
                * back_valid[offset],
                axis=0,
            )
            for offset in range(kernel)
        ]
    )
    grad_product = tap_values[0] * grad_conv_wide * ahead_valid[0]
    for offset in range(1, kernel):
        grad_product = (
            grad_product
            + tap_values[offset] * trailing[offset : offset + tok_rows] * ahead_valid[offset]
        )
    grad_streams = jnp.stack([grad_product * streams[2], grad_c, grad_product * streams[0]]).astype(
        jnp.bfloat16
    )
    stream_part = jnp.einsum(
        "td,stc->sdc", normed_one, grad_streams, preferred_element_type=jnp.float32
    )
    normed_one_part = jnp.einsum(
        "stc,sdc->td", grad_streams, stream_weight, preferred_element_type=jnp.float32
    )
    grad_normed_one = lax.psum(normed_one_part, "tensor")
    gain_one_part = jnp.sum(grad_normed_one * normal_one, axis=0)
    input_grad = grad_middle + norm_back(grad_normed_one, normal_one, scale_one, gain_pair[0])
    gain_stack = jnp.stack([gain_one_part, gain_two_part])
    gains_grad, taps_grad = lax.psum((gain_stack, taps_part), "dp")
    stream_total, mixer_total, hidden_total, down_total = (
        lax.psum_scatter(stream_part, "dp", scatter_dimension=1, tiled=True),
        lax.psum_scatter(mixer_part, "dp", scatter_dimension=1, tiled=True),
        lax.psum_scatter(hidden_part, "dp", scatter_dimension=1, tiled=True),
        lax.psum_scatter(down_part, "dp", scatter_dimension=1, tiled=True),
    )
    first_dp = (lax.axis_index("dp") == 0).astype(jnp.float32)
    first_tensor = (lax.axis_index("tensor") == 0).astype(jnp.float32)
    local_square = (
        squares(stream_total) + squares(mixer_total) + squares(hidden_total) + squares(down_total)
    )
    local_square = local_square + first_dp * (
        squares(taps_grad) + first_tensor * squares(gains_grad)
    )
    square_total = lax.psum(local_square, ("dp", "tensor"))
    grad_norm = jnp.sqrt(square_total)
    factor = jnp.minimum(1.0, CLIP_NORM / (grad_norm + 1e-06))
    gains_out = adam_step(gain_pair, gains_grad, gains_first, gains_second, factor, 0.0)
    taps_out = adam_step(tap_values, taps_grad, taps_first, taps_second, factor, DECAY_RATE)
    stream_out = adam_step(
        own_share(stream_weight, stream_total.shape[1]),
        stream_total,
        stream_first,
        stream_second,
        factor,
        DECAY_RATE,
    )
    mixer_out = adam_step(
        own_share(mixer_weight, mixer_total.shape[1]),
        mixer_total,
        mixer_first,
        mixer_second,
        factor,
        DECAY_RATE,
    )
    hidden_out = adam_step(
        own_share(hidden_weight, hidden_total.shape[1]),
        hidden_total,
        hidden_first,
        hidden_second,
        factor,
        DECAY_RATE,
    )
    down_out = adam_step(
        own_share(down_weight, down_total.shape[1]),
        down_total,
        down_first,
        down_second,
        factor,
        DECAY_RATE,
    )
    return (
        block_out,
        input_grad,
        grad_norm,
        gains_grad,
        gains_out[0],
        gains_out[1],
        gains_out[2],
        taps_grad,
        taps_out[0],
        taps_out[1],
        taps_out[2],
        stream_total,
        stream_out[0],
        stream_out[1],
        stream_out[2],
        mixer_total,
        mixer_out[0],
        mixer_out[1],
        mixer_out[2],
        hidden_total,
        hidden_out[0],
        hidden_out[1],
        hidden_out[2],
        down_total,
        down_out[0],
        down_out[1],
        down_out[2],
    )


def solution(mesh):
    return jax.shard_map(
        body,
        mesh=mesh,
        in_specs=(
            P("dp", None),
            P(),
            P("dp", None),
            P(),
            P(None, "tensor"),
            P(None, None, "tensor"),
            P("tensor", None),
            P(None, None, "tensor"),
            P("tensor", None),
            P(),
            P(),
            P(None, "tensor"),
            P(None, "tensor"),
            P(None, "dp", "tensor"),
            P(None, "dp", "tensor"),
            P("tensor", "dp"),
            P("tensor", "dp"),
            P(None, "dp", "tensor"),
            P(None, "dp", "tensor"),
            P("tensor", "dp"),
            P("tensor", "dp"),
        ),
        out_specs=(
            P("dp", None),
            P("dp", None),
            P(),
            P(),
            P(),
            P(),
            P(),
            P(None, "tensor"),
            P(None, "tensor"),
            P(None, "tensor"),
            P(None, "tensor"),
            P(None, "dp", "tensor"),
            P(None, "dp", "tensor"),
            P(None, "dp", "tensor"),
            P(None, "dp", "tensor"),
            P("tensor", "dp"),
            P("tensor", "dp"),
            P("tensor", "dp"),
            P("tensor", "dp"),
            P(None, "dp", "tensor"),
            P(None, "dp", "tensor"),
            P(None, "dp", "tensor"),
            P(None, "dp", "tensor"),
            P("tensor", "dp"),
            P("tensor", "dp"),
            P("tensor", "dp"),
            P("tensor", "dp"),
        ),
        check_vma=False,
    )
```

profile of v0, /device:TPU:0, one launch (start us, length us, event | category | flops | bytes accessed | tf_op | source)
XLA Modules:
  0.0 1472.9 jit_solution(3615150835446457697)
XLA Ops:
  8.2 3.0 fusion.11
  11.3 4.3 convolution_bitcast_fusion.4
  19.4 3.0 collective-permute-start
  27.3 3.9 multiply_convert_fusion.8
  32.0 4.5 fusion.54
  36.8 224.8 %all-reduce.8.cloned.1.call-done = f32[1024,1536]{1,0:T(8,128)} async-done(((f32[1024,1536]{1,0:T(8,128)}), f32[1024,1536]{1,0:T(8,128)}) %all-reduce.8.cloned.1.call-update) | async-done | bytes 6291472 | tf_op jit(solution)/shard_map/psum | solution.py:123
  261.6 4.6 multiply_reduce_fusion.2
  266.2 2.7 copy-done.2
  268.9 17.3 %convolution_bitcast_fusion.1 = f32[2,1024,1728]{1,2,0:T(8,128)} fusion(bf16[2,1536,1728]{1,2,0:T(8,128)(2,1)} %param.28, f32[1024,1536]{1,0:T(8,128)S(1)} %get-tuple-element.146, f32[1536]{0:T(1024)S(1)} %get-tuple-element.115, f32[1024]{0:T(1024)S(1)} %add_rsqrt_fusion), kind=kOutput, calls=%fused_computation.16 | convolution fusion | flops 10876354560 | bytes 31074304 | tf_op jit(solution)/shard_map/td,sdf->stf/dot_general | solution.py:128
  286.2 16.0 %fusion.15 = (bf16[1,1024,1728]{1,2,0:T(8,128)(2,1)}, bf16[1,1024,1728]{1,2,0:T(8,128)(2,1)}, bf16[1024,1728]{0,1:T(8,128)(2,1)}) fusion(f32[2,1024,1728]{1,2,0:T(8,128)} %convolution_bitcast_fusion.1, bf16[1024,1536]{1,0:T(8,128)(2,1)S(1)} %copy-done.13, bf16[1728,1536]{1,0:T(8,128)(2,1)} %param.29), kind=kOutput, calls=%fused_computation.38 | convolution fusion | flops 5462360064 | bytes 33226752 | tf_op jit(solution)/shard_map/dot_general | solution.py:53
  302.2 16.0 %fusion.13 = f32[1024,1536]{1,0:T(8,128)} fusion(bf16[2,1536,1728]{1,2,0:T(8,128)(2,1)S(1)} %bitcast.95, bf16[1,1024,1728]{1,2,0:T(8,128)(2,1)} %get-tuple-element.150, bf16[1,1024,1728]{1,2,0:T(8,128)(2,1)} %get-tuple-element.149), kind=kOutput, calls=%fused_computation.33 | convolution fusion | flops 10875174912 | bytes 23986176 | tf_op jit(solution)/shard_map/stf,sdf->td/dot_general | solution.py:146
  318.3 10.2 convolution_convert_fusion
  328.5 211.6 %all-reduce.12.cloned.1.call-done = f32[1024,1536]{1,0:T(8,128)} async-done(((f32[1024,1536]{1,0:T(8,128)}), f32[1024,1536]{1,0:T(8,128)}) %all-reduce.12.cloned.1.call-update) | async-done | bytes 6291472 | tf_op jit(solution)/shard_map/psum | solution.py:149
  540.1 6.1 multiply_reduce_fusion
  546.8 116.2 %all-reduce.10.cloned.1.call-done = bf16[1024,1536]{1,0:T(8,128)(2,1)} async-done(((bf16[1024,1536]{1,0:T(8,128)(2,1)}), bf16[1024,1536]{1,0:T(8,128)(2,1)}) %all-reduce.10.cloned.1.call-update) | async-done | bytes 3145744 | tf_op jit(solution)/shard_map/psum | solution.py:135
  663.0 9.4 multiply_add_fusion
  672.4 2.7 copy-done.1
  675.1 3.2 fusion.25
  678.6 19.5 %convolution_bitcast_fusion = f32[2,1536,1728]{1,2,0:T(8,128)} fusion(bf16[1,1024,1728]{1,2,0:T(8,128)(2,1)} %get-tuple-element.150, bf16[1,1024,1728]{1,2,0:T(8,128)(2,1)} %get-tuple-element.149, f32[1024,1536]{1,0:T(8,128)} %copy-done.2, f32[1536]{0:T(1024)S(1)} %get-tuple-element.115, f32[1024]{0:T(1024)S(1)} %add_rsqrt_fusion), kind=kOutput, calls=%fused_computation | convolution fusion | flops 10879893504 | bytes 34613248 | tf_op jit(solution)/shard_map/td,stf->sdf/dot_general | solution.py:143
  698.1 32.6 %copy.83 = f32[2,1536,1728]{2,0,1:T(2,128)} copy(f32[2,1536,1728]{1,2,0:T(8,128)} %convolution_bitcast_fusion) | data formatting | bytes 42467328 | tf_op jit(solution)/shard_map/td,stf->sdf/transpose | solution.py:143
  730.9 5.0 fusion.27
  741.1 3.3 multiply_reduce_fusion.6
  747.3 6.3 convolution_bitcast_fusion.3
  753.6 11.2 fusion.55
  765.5 10.0 convolution_bitcast_fusion.2
  775.4 10.9 copy.97
  786.3 7.3 copy.104
  796.5 2.5 copy.85
  799.0 2.6 copy.84
  805.1 4.0 constant_dynamic-slice_fusion.1
  809.0 2.6 copy.102
  811.7 2.6 constant_dynamic-slice_fusion
  823.4 179.7 %all-reduce.16.cloned.1.call-done = f32[2,1536,1728]{2,0,1:T(2,128)} async-done(((f32[2,1536,1728]{2,0,1:T(2,128)}), f32[2,1536,1728]{2,0,1:T(2,128)}) %all-reduce.16.cloned.1.call-update) | async-done | bytes 21233680
  1003.1 6.7 multiply_reduce_fusion.3
  1009.7 218.6 %all-reduce.14.cloned.1.call-done = f32[1024,1536]{1,0:T(8,128)} async-done(((f32[1024,1536]{1,0:T(8,128)}), f32[1024,1536]{1,0:T(8,128)}) %all-reduce.14.cloned.1.call-update) | async-done | bytes 6291472 | tf_op jit(solution)/shard_map/psum | solution.py:186
  1228.3 4.7 fusion.10
  1233.6 25.3 %all-reduce.1 = (f32[3,384]{1,0:T(4,128)}, f32[2,1536]{1,0:T(2,128)}) all-reduce(f32[3,384]{1,0:T(4,128)} %pad_maximum_fusion.9, f32[2,1536]{1,0:T(2,128)} %pad_maximum_fusion.8), channel_id=1, replica_groups=mesh['dp'=8,'tensor'=4] {'dp'}, use_global_device_ids=true, to_apply=%region_19.0 | all-reduce | flops 4224 | bytes 33792 | tf_op jit(solution)/shard_map/psum | solution.py:190
  1262.9 9.6 fusion.9
  1272.5 43.3 %reduce-scatter.8.cloned.1.call-done = f32[1728,192]{0,1:T(8,128)} async-done(((f32[1728,1536]{0,1:T(8,128)}), f32[1728,192]{0,1:T(8,128)}) %reduce-scatter.8.cloned.1.call-update) | async-done | bytes 1327120 | tf_op jit(solution)/shard_map/reduce_scatter | solution.py:195
  1318.1 66.8 %reduce-scatter.10.cloned.1.call-done = f32[192,1152]{1,0:T(8,128)} async-done(((f32[1536,1152]{1,0:T(8,128)}), f32[192,1152]{1,0:T(8,128)}) %reduce-scatter.10.cloned.1.call-update) | async-done | bytes 884752
  1387.2 2.4 copy.98
  1396.6 39.2 %psum.55 = f32[]{:T(128)} all-reduce(f32[]{:T(128)S(6)} %add.202), channel_id=1, replica_groups=mesh['dp'=8,'tensor'=4] {'dp','tensor'}, use_global_device_ids=true, to_apply=%region_25.0 | all-reduce | flops 1 | bytes 8 | tf_op jit(solution)/shard_map/psum | solution.py:205
  1436.6 4.6 add_multiply_fusion.2
  1441.2 2.6 copy.92
  1443.8 2.5 copy.93
  1446.3 2.5 copy.94
  1451.6 8.9 add_multiply_fusion
  1461.7 2.8 add_multiply_fusion.1
  (148 shorter events, 51.5 us)
Async XLA Ops:
  7.2 4.0 copy-start
  7.2 254.4 %all-reduce.8.cloned.1.call-start = ((), (), s32[]{:S(2)}) async-start(), calls=%async_computation.3 | async-start | bytes 12582912 | tf_op jit(solution)/shard_map/psum | solution.py:123
  7.3 4.0 copy-start.5
  8.2 7.4 copy-start.24
  11.2 4.3 copy-start.29
  15.6 2.2 copy-start.6
  17.8 4.6 copy-start.38
  19.4 6.6 collective-permute-start
  23.0 8.2 copy-start.32
  26.0 5.2 copy-start.27
  27.3 3.9 copy-start.3
  27.3 4.8 copy-start.10
  36.6 503.5 %all-reduce.12.cloned.1.call-start = ((), (), s32[]{:S(2)}) async-start(), calls=%async_computation.5 | async-start | bytes 12582912 | tf_op jit(solution)/shard_map/psum | solution.py:149
  266.2 2.7 copy-start.2
  268.9 17.3 %copy-start.13 = (bf16[1024,1536]{1,0:T(8,128)(2,1)S(1)}, bf16[1024,1536]{1,0:T(8,128)(2,1)}, u32[]{:S(2)}) copy-start(bf16[1024,1536]{1,0:T(8,128)(2,1)} %param.23) | copy-start | bytes 9437188
  268.9 33.3 %slice-start = ((s8[10616832]{0:T(1024)(128)(4,1)}), s8[2228224]{0:T(1024)(128)(4,1)S(1)}, s32[]{:S(2)}) async-start(s8[10616832]{0:T(1024)(128)(4,1)} %bitcast.94), calls=%async_computation.11 | async-start | bytes 4456448
  268.9 33.3 %slice-start.1 = ((s8[10616832]{0:T(1024)(128)(4,1)}), s8[4194304]{0:T(1024)(128)(4,1)S(1)}, s32[]{:S(2)}) async-start(s8[10616832]{0:T(1024)(128)(4,1)} %bitcast.94), calls=%async_computation.12 | async-start | bytes 8388608
  286.2 16.0 %slice-start.2 = ((s8[10616832]{0:T(1024)(128)(4,1)}), s8[4194304]{0:T(1024)(128)(4,1)S(1)}, s32[]{:S(2)}) async-start(s8[10616832]{0:T(1024)(128)(4,1)} %bitcast.94), calls=%async_computation.13 | async-start | bytes 8388608
  318.2 344.8 %all-reduce.10.cloned.1.call-start = ((), (), s32[]{:S(2)}) async-start(), calls=%async_computation.4 | async-start | bytes 6291456 | tf_op jit(solution)/shard_map/psum | solution.py:135
  328.5 493.3 %reduce-scatter.6.cloned.1.call-start = ((), (), s32[]{:S(2)}) async-start(), calls=%async_computation.7 | async-start | bytes 2654208 | tf_op jit(solution)/shard_map/reduce_scatter | solution.py:193
  663.0 12.1 copy-start.8
  672.4 2.7 copy-start.1
  678.4 324.7 %all-reduce.16.cloned.1.call-start = ((), (), s32[]{:S(2)}) async-start(), calls=%async_computation.10 | async-start | bytes 44040192
  730.8 497.5 %all-reduce.14.cloned.1.call-start = ((), (), s32[]{:S(2)}) async-start(), calls=%async_computation.6 | async-start | bytes 12582912 | tf_op jit(solution)/shard_map/psum | solution.py:186
  730.8 5.0 copy-start.9
  735.9 5.2 copy-start.4
  735.9 5.2 copy-start.28
  735.9 5.2 copy-start.33
  735.9 5.2 copy-start.34
  735.9 5.2 copy-start.35
  735.9 5.2 copy-start.36
  735.9 5.2 copy-start.37
  737.9 8.5 copy-start.18
  737.9 3.1 collective-permute-start.1
  753.5 562.3 %reduce-scatter.8.cloned.1.call-start = ((), (), s32[]{:S(2)}) async-start(), calls=%async_computation.8 | async-start | bytes 12386304 | tf_op jit(solution)/shard_map/reduce_scatter | solution.py:195
  764.8 620.1 %reduce-scatter.10.cloned.1.call-start = ((), (), s32[]{:S(2)}) async-start(), calls=%async_computation.9 | async-start | bytes 7962624
  809.0 12.1 copy-start.40
  1228.3 4.7 copy-start.31
  1441.2 7.6 copy-start.26
  1441.2 9.0 copy-start.39
  1451.6 9.0 copy-start.17
  1451.6 9.0 copy-start.21
  1451.6 9.0 copy-start.22
  1451.6 9.0 copy-start.23
  1451.6 10.1 copy-start.11
  1451.6 10.1 copy-start.14
  1451.6 10.1 copy-start.15
  1451.6 10.0 copy-start.16
  (6 other events, 6.0 us)
Sparse Core Ops, SparseCore 0:
  36.7 224.8 all-reduce.7
  318.3 221.7 all-reduce.11
  543.1 119.9 all-reduce.9
  678.5 41.3 reduce-scatter.5
  730.9 272.1 all-reduce.15
  1005.3 222.9 all-reduce.13
  1232.4 83.3 reduce-scatter.7
  1319.3 65.4 reduce-scatter.9
where the time goes:
time: 1480 us; the launch traced here: 1470 us
  waiting for transfers between devices  1060 us (72%)
  matrix products  123 us (8%)
  local copies, waits for them, and re-layouts  106 us (7%)
  other arithmetic  89.6 us (6%)
  blocking collectives  64.6 us (4%)
  between operations  21.5 us (1%)
    unnamed x10, waiting for transfers between devices  247 us
    psum x1, waiting for transfers between devices, body(): branch = lax.psum(branch_part, 'tensor')  225 us
    psum x1, waiting for transfers between devices, body(): grad_normed_one = lax.psum(normed_one_part, 'tensor')  219 us
    psum x1, waiting for transfers between devices, body(): grad_normed_two = lax.psum(normed_two_part, 'tensor')  212 us
    psum x1, waiting for transfers between devices, body(): lax.psum(feed_part.astype(jnp.bfloat16), 'tensor').astype(jnp.float32)  116 us
    unnamed x103, local copies, waits for them, and re-layouts  58.6 us
    reduce_scatter x1, waiting for transfers between devices, body(): lax.psum_scatter(down_part, 'dp', scatter_dimension=1, tiled=True)  43.3 us
    psum x1, blocking collectives, body(): square_total = lax.psum(local_square, ('dp', 'tensor'))  39.2 us
  transfers between devices with their start and end apart: 10, of which 8 were waited for; matrix products, arithmetic and copies ran while one was open for 13% of the time, Pallas kernels for 0%

commit v1 on v0

--- a/solution.py
+++ b/solution.py
@@ -120,7 +120,8 @@
         )
     gated_rows = (streams[1] * conv_out).astype(jnp.bfloat16)
     branch_part = jnp.dot(gated_rows, mixer_weight, preferred_element_type=jnp.float32)
-    branch = lax.psum(branch_part, "tensor")
+    number_ratios = lambda row_data: jnp.sum(lax.all_gather(row_data, "tensor"), axis=0)
+    branch = number_ratios(branch_part)
     middle = tokens + branch
     scale_two = rms_scale(middle)
     normal_two = middle * scale_two

time: 1480 us -> 1690 us (1.14)
  waiting for transfers between devices: 1060 us -> 1260 us
    all_gather x0 -> x1, waiting for transfers between devices: none -> 427 us  [body(): lax.all_gather(row_data, 'tensor')]
    psum x1 -> x0, waiting for transfers between devices: 225 us -> none  [body(): branch = lax.psum(branch_part, 'tensor')]
  transfers between devices with their start and end apart: 10 -> 10, of which waited for: 8 -> 8; matrix products, arithmetic and copies ran while one was open for 13% -> 11% of each run, Pallas kernels for 0% -> 0%
where the time goes in v1:
time: 1690 us
  waiting for transfers between devices  1260 us (75%)
  matrix products  123 us (7%)
  local copies, waits for them, and re-layouts  106 us (6%)
  other arithmetic  103 us (6%)
  blocking collectives  64.6 us (4%)
  between operations  21.5 us (1%)
    all_gather x1, waiting for transfers between devices, body(): lax.all_gather(row_data, 'tensor')  427 us
    unnamed x10, waiting for transfers between devices  247 us
    psum x1, waiting for transfers between devices, body(): grad_normed_one = lax.psum(normed_one_part, 'tensor')  219 us
    psum x1, waiting for transfers between devices, body(): grad_normed_two = lax.psum(normed_two_part, 'tensor')  211 us
    psum x1, waiting for transfers between devices, body(): lax.psum(feed_part.astype(jnp.bfloat16), 'tensor').astype(jnp.float32)  116 us
    unnamed x103, local copies, waits for them, and re-layouts  58.6 us
    reduce_scatter x1, waiting for transfers between devices, body(): lax.psum_scatter(down_part, 'dp', scatter_dimension=1, tiled=True)  43.3 us
    psum x1, blocking collectives, body(): square_total = lax.psum(local_square, ('dp', 'tensor'))  39.2 us
  transfers between devices with their start and end apart: 10, of which 8 were waited for; matrix products, arithmetic and copies ran while one was open for 11% of the time, Pallas kernels for 0%

profile of v1, /device:TPU:0, one launch (start us, length us, event | category | flops | bytes accessed | tf_op | source)
XLA Modules:
  0.0 1687.6 jit_solution(9208829163664806828)
XLA Ops:
  8.2 3.0 fusion.11
  11.3 4.3 convolution_bitcast_fusion.4
  19.4 3.0 collective-permute-start
  27.3 3.9 multiply_convert_fusion.8
  32.0 4.5 fusion.54
  36.8 427.1 %all-gather.3.cloned.1.call-done = f32[4096,1536]{1,0:T(8,128)} async-done(((f32[1024,1536]{1,0:T(8,128)}), f32[4096,1536]{1,0:T(8,128)}) %all-gather.3.cloned.1.call-update) | async-done | bytes 25165840 | tf_op jit(solution)/shard_map/all_gather | solution.py:123
  463.9 13.2 reduce_sum.145
  477.1 4.6 multiply_reduce_fusion.2
  481.7 2.7 copy-done.2
  484.4 17.3 %convolution_bitcast_fusion.1 = f32[2,1024,1728]{1,2,0:T(8,128)} fusion(bf16[2,1536,1728]{1,2,0:T(8,128)(2,1)} %param.28, f32[1024,1536]{1,0:T(8,128)S(1)} %get-tuple-element.146, f32[1536]{0:T(1024)S(1)} %get-tuple-element.115, f32[1024]{0:T(1024)S(1)} %add_rsqrt_fusion), kind=kOutput, calls=%fused_computation.16 | convolution fusion | flops 10876354560 | bytes 31074304 | tf_op jit(solution)/shard_map/td,sdf->stf/dot_general | solution.py:129
  501.7 16.0 fusion.15
  517.7 16.0 fusion.13
  533.8 10.2 convolution_convert_fusion
  544.0 210.9 %all-reduce.9.cloned.1.call-done = f32[1024,1536]{1,0:T(8,128)} async-done(((f32[1024,1536]{1,0:T(8,128)}), f32[1024,1536]{1,0:T(8,128)}) %all-reduce.9.cloned.1.call-update) | async-done | bytes 6291472 | tf_op jit(solution)/shard_map/psum | solution.py:150
  754.9 6.1 multiply_reduce_fusion
  761.6 116.2 %all-reduce.7.cloned.1.call-done = bf16[1024,1536]{1,0:T(8,128)(2,1)} async-done(((bf16[1024,1536]{1,0:T(8,128)(2,1)}), bf16[1024,1536]{1,0:T(8,128)(2,1)}) %all-reduce.7.cloned.1.call-update) | async-done | bytes 3145744 | tf_op jit(solution)/shard_map/psum | solution.py:136
  877.8 9.4 multiply_add_fusion
  887.2 2.7 copy-done.1
  889.9 3.2 fusion.25
  893.4 19.5 %convolution_bitcast_fusion = f32[2,1536,1728]{1,2,0:T(8,128)} fusion(bf16[1,1024,1728]{1,2,0:T(8,128)(2,1)} %get-tuple-element.150, bf16[1,1024,1728]{1,2,0:T(8,128)(2,1)} %get-tuple-element.149, f32[1024,1536]{1,0:T(8,128)} %copy-done.2, f32[1536]{0:T(1024)S(1)} %get-tuple-element.115, f32[1024]{0:T(1024)S(1)} %add_rsqrt_fusion), kind=kOutput, calls=%fused_computation | convolution fusion | flops 10879893504 | bytes 34613248 | tf_op jit(solution)/shard_map/td,stf->sdf/dot_general | solution.py:144
  912.9 32.7 %copy.83 = f32[2,1536,1728]{2,0,1:T(2,128)} copy(f32[2,1536,1728]{1,2,0:T(8,128)} %convolution_bitcast_fusion) | data formatting | bytes 42467328 | tf_op jit(solution)/shard_map/td,stf->sdf/transpose | solution.py:144
  945.6 5.0 fusion.27
  955.9 3.3 multiply_reduce_fusion.6
  962.1 6.3 convolution_bitcast_fusion.3
  968.4 11.2 fusion.55
  980.3 10.0 convolution_bitcast_fusion.2
  990.2 10.8 copy.97
  1001.1 7.3 copy.104
  1011.3 2.5 copy.85
  1013.8 2.6 copy.84
  1019.9 4.0 constant_dynamic-slice_fusion.1
  1023.8 2.6 copy.102
  1026.4 2.6 constant_dynamic-slice_fusion
  1038.2 179.7 %all-reduce.13.cloned.1.call-done = f32[2,1536,1728]{2,0,1:T(2,128)} async-done(((f32[2,1536,1728]{2,0,1:T(2,128)}), f32[2,1536,1728]{2,0,1:T(2,128)}) %all-reduce.13.cloned.1.call-update) | async-done | bytes 21233680
  1217.9 6.7 multiply_reduce_fusion.3
  1224.5 218.6 %all-reduce.11.cloned.1.call-done = f32[1024,1536]{1,0:T(8,128)} async-done(((f32[1024,1536]{1,0:T(8,128)}), f32[1024,1536]{1,0:T(8,128)}) %all-reduce.11.cloned.1.call-update) | async-done | bytes 6291472 | tf_op jit(solution)/shard_map/psum | solution.py:187
  1443.1 4.7 fusion.10
  1448.4 25.3 %all-reduce.1 = (f32[3,384]{1,0:T(4,128)}, f32[2,1536]{1,0:T(2,128)}) all-reduce(f32[3,384]{1,0:T(4,128)} %pad_maximum_fusion.9, f32[2,1536]{1,0:T(2,128)} %pad_maximum_fusion.8), channel_id=1, replica_groups=mesh['dp'=8,'tensor'=4] {'dp'}, use_global_device_ids=true, to_apply=%region_19.0 | all-reduce | flops 4224 | bytes 33792 | tf_op jit(solution)/shard_map/psum | solution.py:191
  1477.7 9.6 fusion.9
  1487.3 43.3 %reduce-scatter.8.cloned.1.call-done = f32[1728,192]{0,1:T(8,128)} async-done(((f32[1728,1536]{0,1:T(8,128)}), f32[1728,192]{0,1:T(8,128)}) %reduce-scatter.8.cloned.1.call-update) | async-done | bytes 1327120 | tf_op jit(solution)/shard_map/reduce_scatter | solution.py:196
  1532.9 66.8 %reduce-scatter.10.cloned.1.call-done = f32[192,1152]{1,0:T(8,128)} async-done(((f32[1536,1152]{1,0:T(8,128)}), f32[192,1152]{1,0:T(8,128)}) %reduce-scatter.10.cloned.1.call-update) | async-done | bytes 884752
  1611.4 39.2 %psum.47 = f32[]{:T(128)} all-reduce(f32[]{:T(128)S(6)} %add.200), channel_id=1, replica_groups=mesh['dp'=8,'tensor'=4] {'dp','tensor'}, use_global_device_ids=true, to_apply=%region_25.0 | all-reduce | flops 1 | bytes 8 | tf_op jit(solution)/shard_map/psum | solution.py:206
  1651.4 4.6 add_multiply_fusion.2
  1656.0 2.6 copy.92
  1658.5 2.5 copy.93
  1661.1 2.5 copy.94
  1666.4 8.9 add_multiply_fusion
  1676.5 2.8 add_multiply_fusion.1
  (149 shorter events, 54.0 us)
Async XLA Ops:
  7.2 4.0 copy-start
  7.2 456.7 %all-gather.3.cloned.1.call-start = ((), (), s32[]{:S(2)}) async-start(), calls=%async_computation.8 | async-start | bytes 31457280 | tf_op jit(solution)/shard_map/all_gather | solution.py:123
  7.3 4.0 copy-start.5
  8.2 7.4 copy-start.24
  11.2 4.3 copy-start.29
  15.6 2.2 copy-start.6
  17.8 4.6 copy-start.38
  19.4 6.6 collective-permute-start
  23.0 8.2 copy-start.32
  26.0 5.2 copy-start.27
  27.3 3.9 copy-start.3
  27.3 4.8 copy-start.10
  36.6 718.3 %all-reduce.9.cloned.1.call-start = ((), (), s32[]{:S(2)}) async-start(), calls=%async_computation.4 | async-start | bytes 12582912 | tf_op jit(solution)/shard_map/psum | solution.py:150
  481.7 2.7 copy-start.2
  484.4 17.3 %copy-start.13 = (bf16[1024,1536]{1,0:T(8,128)(2,1)S(1)}, bf16[1024,1536]{1,0:T(8,128)(2,1)}, u32[]{:S(2)}) copy-start(bf16[1024,1536]{1,0:T(8,128)(2,1)} %param.23) | copy-start | bytes 9437188
  484.4 33.3 %slice-start = ((s8[10616832]{0:T(1024)(128)(4,1)}), s8[2228224]{0:T(1024)(128)(4,1)S(1)}, s32[]{:S(2)}) async-start(s8[10616832]{0:T(1024)(128)(4,1)} %bitcast.96), calls=%async_computation.11 | async-start | bytes 4456448
  484.4 33.3 %slice-start.1 = ((s8[10616832]{0:T(1024)(128)(4,1)}), s8[4194304]{0:T(1024)(128)(4,1)S(1)}, s32[]{:S(2)}) async-start(s8[10616832]{0:T(1024)(128)(4,1)} %bitcast.96), calls=%async_computation.12 | async-start | bytes 8388608
  501.7 16.0 slice-start.2
  533.7 344.1 %all-reduce.7.cloned.1.call-start = ((), (), s32[]{:S(2)}) async-start(), calls=%async_computation.3 | async-start | bytes 6291456 | tf_op jit(solution)/shard_map/psum | solution.py:136
  544.0 492.6 %reduce-scatter.6.cloned.1.call-start = ((), (), s32[]{:S(2)}) async-start(), calls=%async_computation.6 | async-start | bytes 2654208 | tf_op jit(solution)/shard_map/reduce_scatter | solution.py:194
  877.8 12.1 copy-start.8
  887.2 2.7 copy-start.1
  893.2 324.7 %all-reduce.13.cloned.1.call-start = ((), (), s32[]{:S(2)}) async-start(), calls=%async_computation.10 | async-start | bytes 44040192
  945.6 497.5 %all-reduce.11.cloned.1.call-start = ((), (), s32[]{:S(2)}) async-start(), calls=%async_computation.5 | async-start | bytes 12582912 | tf_op jit(solution)/shard_map/psum | solution.py:187
  945.6 5.0 copy-start.9
  950.7 5.2 copy-start.4
  950.7 5.2 copy-start.28
  950.7 5.2 copy-start.33
  950.7 5.2 copy-start.34
  950.7 5.2 copy-start.35
  950.7 5.2 copy-start.36
  950.7 5.2 copy-start.37
  952.7 8.5 copy-start.18
  952.7 3.1 collective-permute-start.1
  968.3 562.3 %reduce-scatter.8.cloned.1.call-start = ((), (), s32[]{:S(2)}) async-start(), calls=%async_computation.7 | async-start | bytes 12386304 | tf_op jit(solution)/shard_map/reduce_scatter | solution.py:196
  979.6 620.1 %reduce-scatter.10.cloned.1.call-start = ((), (), s32[]{:S(2)}) async-start(), calls=%async_computation.9 | async-start | bytes 7962624
  1023.8 12.1 copy-start.40
  1443.1 4.7 copy-start.31
  1656.0 7.6 copy-start.26
  1656.0 9.0 copy-start.39
  1666.4 9.0 copy-start.17
  1666.4 9.0 copy-start.21
  1666.4 9.0 copy-start.22
  1666.4 9.0 copy-start.23
  1666.4 10.1 copy-start.11
  1666.4 10.1 copy-start.14
  1666.4 10.1 copy-start.15
  1666.4 10.0 copy-start.16
  (6 other events, 6.0 us)
Sparse Core Ops, SparseCore 0:
  36.7 427.1 all-gather.2
  533.8 221.0 all-reduce.8
  757.8 119.9 all-reduce.6
  893.3 41.3 reduce-scatter.5
  945.7 272.1 all-reduce.12
  1220.1 222.9 all-reduce.10
  1447.2 83.3 reduce-scatter.7
  1534.1 65.4 reduce-scatter.9
